TPU v7x, 256 devices: a whole 4x4x8 slice. The times are simulated.
256 devices in a mesh: dp: 16 (over z, x_lo), rep: 4 (over y), ind: 4 (over x_hi, core).
Axes of the slice: x: 4 (x_hi: 2, x_lo: 2; x = x_hi * 2 + x_lo), y: 4, z: 8, core: 2. Of those that a mesh axis runs over, the one named last changes fastest.
Arguments:
- points: bfloat16 [49152, 64], P(('dp', 'rep')), may hold values from -6 to 6
- targets: float32 [49152], P(('dp', 'rep')), may hold values from -6 to 6
- inducing: float32 [4096, 64], P('ind'), may hold values from -6 to 6
- whitening: bfloat16 [4096, 4096], P('ind'), may hold values from -0.01953125 to 0.01953125
- mean_v: float32 [4096], P('ind'), may hold values from -12 to 12
- covariance: float32 [4096, 4096], P('ind', ('dp', 'rep')), may hold values from -24 to 24
- precision: float32 [4096, 4096], P('ind', ('dp', 'rep')), may hold values from -3 to 3
- natural_one: float32 [4096], P('ind'), may hold values from -6 to 6
- lengthscales: float32 [64], replicated, may hold values from 1.6 to 24
- hypers: float32 [2], replicated, may hold values from 0.5 to 2
Outputs:
- precision_new: float32 [4096, 4096], P('ind', ('dp', 'rep'))
- natural_new: float32 [4096], P('ind')
- expected_fit: float32 [], replicated
All inputs are finite; a program needn't handle non-finite values.
Results may differ from a plain program's by a relative error of at most 0.0076.
Values may be sent and summed in bfloat16 or wider, within the bound.
A program may use at most 128 MiB of HBM per device.

v0:
```python
import functools
import jax
import jax.numpy as jnp
from jax import lax
from jax.sharding import Mesh
from jax.sharding import PartitionSpec as P

IND = ("ind_0", "ind_1")
DP_REP = ("dp_0", "dp_1", "rep")
DP_REP_IND = ("dp_0", "dp_1", "rep", "ind_0", "ind_1")


def joined_along(blocks, dim):
    shape = list(blocks.shape[1:])
    shape[dim] *= blocks.shape[0]
    return jnp.moveaxis(blocks, 0, dim).reshape(shape)


def sent_to_all(array, axis):
    copies = jnp.broadcast_to(array, (lax.axis_size(axis), *array.shape))
    return lax.all_to_all(copies, axis, split_axis=0, concat_axis=0, tiled=True)


def collect(array, axis, dim):
    return joined_along(sent_to_all(array, axis), dim)


def of_everyone(array, axis):
    return sent_to_all(array, axis).sum(axis=0)


def together(arrays, axis):
    ends = [0]
    for a in arrays:
        ends.append(ends[-1] + a.size)
    total = of_everyone(jnp.concatenate([a.ravel() for a in arrays]), axis)
    return tuple((total[b:e].reshape(a.shape) for a, b, e in zip(arrays, ends, ends[1:])))


def sum_in_order(blocks, axes, sequence):
    inside = blocks.shape[1:]
    blocks = blocks.reshape(*(lax.axis_size(a) for a in axes), *inside)
    blocks = jnp.moveaxis(blocks, sequence, range(len(axes))).reshape(-1, *inside)
    for k in sequence:
        blocks = lax.psum_scatter(blocks, axes[k], scatter_dimension=0, tiled=True)
    return blocks[0]


def cut_along(array, dim, length):
    before, after = (array.shape[:dim], array.shape[dim + 1 :])
    return jnp.moveaxis(array.reshape(*before, length, -1, *after), dim, 0)


def summed_rows(array, axes, sequence, dim):
    length = lax.axis_size(axes)
    return sum_in_order(cut_along(array, dim, length), axes, sequence)


def one_axis_at_a_time(array, axes):
    return functools.reduce(lax.psum, axes, array)


def cross_cov(inducing, points, lengthscales, signal):
    scaled_z = inducing / lengthscales
    scaled_x = points.astype(jnp.float32) / lengthscales
    norm_z = jnp.sum(scaled_z * scaled_z, axis=1)
    norm_x = jnp.sum(scaled_x * scaled_x, axis=1)
    inner = jnp.dot(scaled_z, scaled_x.T, precision=lax.Precision.HIGHEST)
    return (signal * jnp.exp(-0.5 * (norm_z[:, None] + norm_x[None, :] - 2.0 * inner))).astype(
        jnp.bfloat16
    )


def shards(
    points,
    targets,
    inducing,
    whitening,
    mean_v,
    covariance,
    precision,
    natural_one,
    lengthscales,
    hypers,
):
    signal = hypers[0]
    noise_var = hypers[1]
    all_inducing = collect(inducing, IND, 0)
    cross = cross_cov(all_inducing, points, lengthscales, signal)
    white = jnp.dot(whitening, cross, preferred_element_type=jnp.float32).astype(jnp.bfloat16)
    white_wide = white.astype(jnp.float32)
    mean_part = jnp.dot(mean_v, white_wide, precision=lax.Precision.HIGHEST)
    square_part = jnp.sum(white_wide * white_wide, axis=0)
    gram_part = lax.dot_general(
        white,
        lax.all_gather(white, IND, axis=0, tiled=True),
        (((1,), (1,)), ((), ())),
        preferred_element_type=jnp.float32,
    )
    pred_mean, sq_norm = together((mean_part, square_part), IND)
    resid = targets - pred_mean
    local_fit = jnp.sum(resid * resid + signal - sq_norm)
    local_proj = jnp.dot(white_wide, targets, precision=lax.Precision.HIGHEST)
    proj, fit_sum = together((local_proj, local_fit), DP_REP)
    own_rows = gram_part.shape[0]
    gram = summed_rows(gram_part.astype(jnp.bfloat16), DP_REP, (2, 0, 1), 1).astype(jnp.float32)
    own_cols = gram.shape[1]
    trace = one_axis_at_a_time(jnp.sum(covariance * gram), DP_REP_IND)
    total = points.shape[0] * lax.axis_size(DP_REP)
    expected_fit = -0.5 * jnp.log(2.0 * jnp.pi * noise_var) - (fit_sum + trace) / (
        2.0 * noise_var * total
    )
    row_ids = lax.axis_index(IND) * own_rows + jnp.arange(own_rows, dtype=jnp.int32)
    col_ids = lax.axis_index(DP_REP) * own_cols + jnp.arange(own_cols, dtype=jnp.int32)
    identity = (row_ids[:, None] == col_ids[None, :]).astype(jnp.float32)
    precision_new = 0.5 * precision + 0.5 * (identity + gram / noise_var)
    natural_new = 0.5 * natural_one + 0.5 * proj / noise_var
    return (precision_new, natural_new, expected_fit)


def solution(mesh):
    finer = Mesh(
        mesh.devices.reshape(8, 2, mesh.shape["rep"], 2, 2),
        ("dp_0", "dp_1", "rep", "ind_0", "ind_1"),
    )
    return jax.shard_map(
        shards,
        mesh=finer,
        in_specs=(
            P(DP_REP, None),
            P(DP_REP),
            P(IND, None),
            P(IND, None),
            P(IND),
            P(IND, DP_REP),
            P(IND, DP_REP),
            P(IND),
            P(),
            P(),
        ),
        out_specs=(P(IND, DP_REP), P(IND), P()),
        check_vma=False,
    )
```

profile of v0, /device:TPU:1, one launch (start us, length us, event | category | flops | bytes accessed | tf_op | source)
XLA Modules:
  0.0 345.0 jit_solution(10306386077363218680)
XLA Ops:
  7.2 2.1 broadcast_in_dim.6
  9.3 6.7 %all-to-all-start = ((f32[4,1024,64]{1,2,0:T(8,128)}), f32[4,1024,64]{1,2,0:T(8,128)S(1)}, u32[]{:S(2)}, u32[]{:S(2)}) async-start(f32[4,1024,64]{1,2,0:T(8,128)} %broadcast_in_dim.6), calls=%async_computation | async-start | bytes 2097152 | tf_op jit(solution)/shard_map/all_to_all | solution.py:21
  16.0 1.3 fusion.15
  17.3 1.0 multiply_reduce_fusion.2
  18.3 12.7 %all-to-all-done = f32[4,1024,64]{1,2,0:T(8,128)S(1)} async-done(((f32[4,1024,64]{1,2,0:T(8,128)}), f32[4,1024,64]{1,2,0:T(8,128)S(1)}, u32[]{:S(2)}, u32[]{:S(2)}) %all-to-all-start) | async-done | bytes 1048608 | tf_op jit(solution)/shard_map/all_to_all | solution.py:21
  31.0 0.9 multiply_reduce_fusion.1
  32.0 13.6 %multiply_convert_fusion = bf16[4096,768]{1,0:T(8,128)(2,1)S(1)} fusion(f32[768]{0:T(1024)S(1)} %multiply_reduce_fusion.2, f32[4096]{0:T(1024)S(1)} %bitcast.44, f32[]{:T(128)} %bitcast, f32[4096,64]{0,1:T(8,128)S(1)} %bitcast.41, f32[64]{0:T(128)S(1)} %copy-done.7, bf16[768,64]{0,1:T(8,128)(2,1)S(1)} %copy-done.4), kind=kOutput, calls=%fused_computation | convolution fusion | flops 2435153920 | bytes 7458052 | tf_op jit(solution)/shard_map/dot_general | solution.py:68
  45.6 7.9 %multiply_reduce_fusion = (f32[768]{0:T(1024)S(1)}, bf16[768,1024]{1,0:T(8,128)(2,1)}) fusion(bf16[4096,768]{1,0:T(8,128)(2,1)S(1)} %multiply_convert_fusion, bf16[1024,4096]{1,0:T(8,128)(2,1)S(1)} %bitcast.46), kind=kOutput, calls=%fused_computation.2 | convolution fusion | flops 6445595648 | bytes 16256000 | tf_op jit(solution)/shard_map/dot_general | solution.py:90
  53.8 53.3 %all-gather.2.cloned.1.call-done = bf16[4096,768]{0,1:T(8,128)(2,1)} async-done(((bf16[1024,768]{0,1:T(8,128)(2,1)}), bf16[4096,768]{0,1:T(8,128)(2,1)}) %all-gather.2.cloned.1.call-update) | async-done | bytes 6291472 | tf_op jit(solution)/shard_map/all_gather | solution.py:96
  107.1 11.3 %convolution_convert_fusion = bf16[1024,4096]{1,0:T(8,128)(2,1)} fusion(bf16[768,1024]{1,0:T(8,128)(2,1)} %get-tuple-element.8, bf16[4096,768]{0,1:T(8,128)(2,1)} %all-gather.2.cloned.1.call-done), kind=kOutput, calls=%fused_computation.1 | convolution fusion | flops 6446645248 | bytes 16252928 | tf_op jit(solution)/shard_map/dot_general | solution.py:94
  118.4 11.9 %copy.27 = bf16[1024,4096]{0,1:T(8,128)(2,1)} copy(bf16[1024,4096]{1,0:T(8,128)(2,1)} %convolution_convert_fusion) | data formatting | bytes 16777216 | tf_op jit(solution)/shard_map/convert_element_type | solution.py:106
  130.3 8.4 %copy.28 = bf16[4,8,2,1024,64]{3,4,2,1,0:T(8,128)(2,1)} copy(bf16[4,8,2,1024,64]{3,4,0,2,1:T(8,128)(2,1)} %bitcast.38) | data formatting | bytes 16777216 | tf_op jit(solution)/shard_map/transpose | solution.py:43
  138.8 82.2 %reduce-scatter.4.cloned.1.call-done = bf16[16,1024,64]{1,2,0:T(8,128)(2,1)} async-done(((bf16[64,1024,64]{1,2,0:T(8,128)(2,1)}), bf16[16,1024,64]{1,2,0:T(8,128)(2,1)}) %reduce-scatter.4.cloned.1.call-update) | async-done | bytes 2097168 | tf_op jit(solution)/shard_map/reduce_scatter | solution.py:45
  221.1 1.3 convolution_reduce_fusion
  222.5 0.6 broadcast_in_dim.7
  223.1 5.0 %all-to-all-start.1 = ((f32[4,1,1536]{2,1,0:T(1,128)}), f32[4,1,1536]{2,1,0:T(1,128)S(1)}, u32[]{:S(2)}, u32[]{:S(2)}) async-start(f32[4,1,1536]{2,1,0:T(1,128)} %broadcast_in_dim.7), calls=%async_computation.4 | async-start | bytes 49152 | tf_op jit(solution)/shard_map/all_to_all | solution.py:21
  228.1 33.8 %reduce-scatter.6.cloned.1.call-done = bf16[2,1024,64]{1,2,0:T(8,128)(2,1)} async-done(((bf16[16,1024,64]{1,2,0:T(8,128)(2,1)}), bf16[2,1024,64]{1,2,0:T(8,128)(2,1)}) %reduce-scatter.6.cloned.1.call-update) | async-done | bytes 262160 | tf_op jit(solution)/shard_map/reduce_scatter | solution.py:45
  261.9 0.7 fusion.13
  262.7 1.2 fusion.9
  263.9 0.6 pad_maximum_fusion.1
  264.6 0.9 broadcast_in_dim.8
  265.5 9.2 %all-to-all-start.2 = ((f32[64,1,1025]{2,1,0:T(1,128)}), f32[64,1,1025]{2,1,0:T(1,128)S(1)}, u32[]{:S(2)}, u32[]{:S(2)}) async-start(f32[64,1,1025]{2,1,0:T(1,128)} %broadcast_in_dim.8), calls=%async_computation.5 | async-start | bytes 589824 | tf_op jit(solution)/shard_map/all_to_all | solution.py:21
  276.0 9.2 %reduce-scatter.8.cloned.1.call-done = bf16[1,1024,64]{1,2,0:T(8,128)(2,1)} async-done(((bf16[2,1024,64]{1,2,0:T(8,128)(2,1)}), bf16[1,1024,64]{1,2,0:T(8,128)(2,1)}) %reduce-scatter.8.cloned.1.call-update) | async-done | bytes 131088 | tf_op jit(solution)/shard_map/reduce_scatter | solution.py:45
  285.2 3.0 fusion.5
  288.2 14.0 %psum.35 = f32[]{:T(128)} all-reduce(f32[]{:T(128)} %get-tuple-element.3), channel_id=1, replica_groups=mesh['dp_0'=8,'dp_1'=2,'rep'=4,'ind_0'=2,'ind_1'=2] {'dp_0'}, use_global_device_ids=true, to_apply=%region_10.0 | all-reduce | flops 1 | bytes 8 | tf_op jit(solution)/shard_map/psum | solution.py:60
  302.2 4.4 %psum.36 = f32[]{:T(128)} all-reduce(f32[]{:T(128)} %psum.35), channel_id=1, replica_groups=mesh['dp_0'=8,'dp_1'=2,'rep'=4,'ind_0'=2,'ind_1'=2] {'dp_1'}, use_global_device_ids=true, to_apply=%region_11.0 | all-reduce | flops 1 | bytes 8 | tf_op jit(solution)/shard_map/psum | solution.py:60
  306.6 0.2 reduce_sum.68
  306.8 9.5 %psum.37 = f32[]{:T(128)} all-reduce(f32[]{:T(128)} %psum.36), channel_id=1, replica_groups=mesh['dp_0'=8,'dp_1'=2,'rep'=4,'ind_0'=2,'ind_1'=2] {'rep'}, use_global_device_ids=true, to_apply=%region_12.0 | all-reduce | flops 1 | bytes 8 | tf_op jit(solution)/shard_map/psum | solution.py:60
  316.4 1.2 fusion.8
  317.6 6.0 %psum.38 = f32[]{:T(128)} all-reduce(f32[]{:T(128)} %psum.37), channel_id=1, replica_groups=mesh['dp_0'=8,'dp_1'=2,'rep'=4,'ind_0'=2,'ind_1'=2] {'ind_0'}, use_global_device_ids=true, to_apply=%region_13.0 | all-reduce | flops 1 | bytes 8 | tf_op jit(solution)/shard_map/psum | solution.py:60
  323.6 0.5 slice.27
  324.1 11.8 %psum.39 = f32[]{:T(128)} all-reduce(f32[]{:T(128)} %psum.38), channel_id=1, replica_groups=mesh['dp_0'=8,'dp_1'=2,'rep'=4,'ind_0'=2,'ind_1'=2] {'ind_1'}, use_global_device_ids=true, to_apply=%region_14.0 | all-reduce | flops 1 | bytes 8 | tf_op jit(solution)/shard_map/psum | solution.py:60
  (38 shorter events, 0.5 us)
Async XLA Ops:
  7.2 213.9 %copy-start = (f32[1024]{0:T(1024)S(1)}, f32[1024]{0:T(1024)}, u32[]{:S(2)}) copy-start(f32[1024]{0:T(1024)} %param.14) | copy-start | bytes 12292
  7.2 24.7 %copy-start.7 = (f32[64]{0:T(128)S(1)}, f32[64]{0:T(128)}, u32[]{:S(2)}) copy-start(f32[64]{0:T(128)} %param.18) | copy-start | bytes 772
  7.2 24.7 %copy-start.4 = (bf16[768,64]{0,1:T(8,128)(2,1)S(1)}, bf16[768,64]{0,1:T(8,128)(2,1)}, u32[]{:S(2)}) copy-start(bf16[768,64]{0,1:T(8,128)(2,1)} %param.10) | copy-start | bytes 294916
  9.3 21.7 %all-to-all-start = ((f32[4,1024,64]{1,2,0:T(8,128)}), f32[4,1024,64]{1,2,0:T(8,128)S(1)}, u32[]{:S(2)}, u32[]{:S(2)}) async-start(f32[4,1024,64]{1,2,0:T(8,128)} %broadcast_in_dim.6), calls=%async_computation | async-start | bytes 2097152 | tf_op jit(solution)/shard_map/all_to_all | solution.py:21
  16.0 91.1 %all-gather.2.cloned.1.call-start = ((), (), s32[]{:S(2)}) async-start(), calls=%async_computation.6 | async-start | bytes 7864320 | tf_op jit(solution)/shard_map/all_gather | solution.py:96
  31.8 13.7 %slice-start = ((s8[8388608]{0:T(1024)(128)(4,1)}), s8[4194304]{0:T(1024)(128)(4,1)S(1)}, s32[]{:S(2)}) async-start(s8[8388608]{0:T(1024)(128)(4,1)} %bitcast.45), calls=%async_computation.10 | async-start | bytes 8388608
  31.9 13.6 %slice-start.1 = ((s8[8388608]{0:T(1024)(128)(4,1)}), s8[4194304]{0:T(1024)(128)(4,1)S(1)}, s32[]{:S(2)}) async-start(s8[8388608]{0:T(1024)(128)(4,1)} %bitcast.45), calls=%async_computation.11 | async-start | bytes 8388608
  53.6 167.5 %reduce-scatter.4.cloned.1.call-start = ((), (), s32[]{:S(2)}) async-start(), calls=%async_computation.7 | async-start | bytes 10485760 | tf_op jit(solution)/shard_map/reduce_scatter | solution.py:45
  138.7 82.3 %copy-start.5 = (f32[768]{0:T(1024)S(1)}, f32[768]{0:T(1024)}, u32[]{:S(2)}) copy-start(f32[768]{0:T(1024)} %param.11) | copy-start | bytes 9220
  138.7 82.4 %copy-start.1 = (bf16[768,1024]{1,0:T(8,128)(2,1)S(1)}, bf16[768,1024]{1,0:T(8,128)(2,1)}, u32[]{:S(2)}) copy-start(bf16[768,1024]{1,0:T(8,128)(2,1)} %get-tuple-element.8) | copy-start | bytes 4718596
  138.7 146.5 %copy-start.2 = (f32[1024,64]{0,1:T(8,128)S(1)}, f32[1024,64]{0,1:T(8,128)}, u32[]{:S(2)}) copy-start(f32[1024,64]{0,1:T(8,128)} %param.15) | copy-start | bytes 786436
  138.7 146.5 %copy-start.3 = (f32[1024,64]{0,1:T(8,128)S(1)}, f32[1024,64]{0,1:T(8,128)}, u32[]{:S(2)}) copy-start(f32[1024,64]{0,1:T(8,128)} %param.16) | copy-start | bytes 786436
  138.7 177.6 %copy-start.6 = (f32[1024]{0:T(1024)S(1)}, f32[1024]{0:T(1024)}, u32[]{:S(2)}) copy-start(f32[1024]{0:T(1024)} %param.17) | copy-start | bytes 12292
  138.8 123.1 %reduce-scatter.6.cloned.1.call-start = ((), (), s32[]{:S(2)}) async-start(), calls=%async_computation.8 | async-start | bytes 2359296 | tf_op jit(solution)/shard_map/reduce_scatter | solution.py:45
  223.1 39.6 %all-to-all-start.1 = ((f32[4,1,1536]{2,1,0:T(1,128)}), f32[4,1,1536]{2,1,0:T(1,128)S(1)}, u32[]{:S(2)}, u32[]{:S(2)}) async-start(f32[4,1,1536]{2,1,0:T(1,128)} %broadcast_in_dim.7), calls=%async_computation.4 | async-start | bytes 49152 | tf_op jit(solution)/shard_map/all_to_all | solution.py:21
  228.1 57.1 %reduce-scatter.8.cloned.1.call-start = ((), (), s32[]{:S(2)}) async-start(), calls=%async_computation.9 | async-start | bytes 393216 | tf_op jit(solution)/shard_map/reduce_scatter | solution.py:45
  265.5 41.2 %all-to-all-start.2 = ((f32[64,1,1025]{2,1,0:T(1,128)}), f32[64,1,1025]{2,1,0:T(1,128)S(1)}, u32[]{:S(2)}, u32[]{:S(2)}) async-start(f32[64,1,1025]{2,1,0:T(1,128)} %broadcast_in_dim.8), calls=%async_computation.5 | async-start | bytes 589824 | tf_op jit(solution)/shard_map/all_to_all | solution.py:21
Sparse Core Ops, SparseCore 0:
  53.7 53.3 all-gather.1
  138.9 82.1 reduce-scatter.3
  223.6 38.2 reduce-scatter.5
  264.2 20.9 reduce-scatter.7
where the time goes:
time: 346 us; the launch traced here: 345 us
  waiting for transfers between devices  191 us (55%)
  blocking collectives  45.7 us (13%)
  matrix products  34.9 us (10%)
  local copies, waits for them, and re-layouts  25.9 us (7%)
  starting transfers between devices  21.1 us (6%)
  between operations  17.8 us (5%)
  other arithmetic  8.27 us (2%)
    reduce_scatter x3, waiting for transfers between devices, sum_in_order(): blocks = lax.psum_scatter(blocks, axes[k], scatter_dimension=0, tiled=True)  125 us
    all_gather x1, waiting for transfers between devices, shards(): lax.all_gather(white, IND, axis=0, tiled=True)  53.3 us
    psum x5, blocking collectives, one_axis_at_a_time(): return functools.reduce(lax.psum, axes, array)  45.7 us
    all_to_all x3, starting transfers between devices, sent_to_all(): return lax.all_to_all(copies, axis, split_axis=0, concat_axis=0, tiled=True)  20.8 us
    dot_general x1, matrix products, cross_cov(): inner = jnp.dot(scaled_z, scaled_x.T, precision=lax.Precision.HIGHEST)  13.6 us
    all_to_all x3, waiting for transfers between devices, sent_to_all(): return lax.all_to_all(copies, axis, split_axis=0, concat_axis=0, tiled=True)  12.7 us
    convert_element_type x1, local copies, waits for them, and re-layouts, shards(): gram_part.astype(jnp.bfloat16)  11.9 us
    dot_general x1, matrix products, shards(): lax.dot_general(white, lax.all_gather(white, IND, axis=0, tiled=True), ((...  11.3 us
  transfers between devices with their start and end apart: 7, of which 5 were waited for; matrix products, arithmetic and copies ran while one was open for 3% of the time, Pallas kernels for 0%

commit v1 on v0

--- a/solution.py
+++ b/solution.py
@@ -91,11 +91,12 @@
     white_wide = white.astype(jnp.float32)
     mean_part = jnp.dot(mean_v, white_wide, precision=lax.Precision.HIGHEST)
     square_part = jnp.sum(white_wide * white_wide, axis=0)
+    make_digits_all = lambda local_block: jnp.concatenate(
+        lax.all_to_all(jnp.stack([local_block for _ in range(lax.axis_size(IND))]), IND, 0, 0),
+        axis=0,
+    )
     gram_part = lax.dot_general(
-        white,
-        lax.all_gather(white, IND, axis=0, tiled=True),
-        (((1,), (1,)), ((), ())),
-        preferred_element_type=jnp.float32,
+        white, make_digits_all(white), (((1,), (1,)), ((), ())), preferred_element_type=jnp.float32
     )
     pred_mean, sq_norm = together((mean_part, square_part), IND)
     resid = targets - pred_mean

time: 346 us -> 366 us (1.058)
  blocking collectives: 45.7 us -> 120 us
  waiting for transfers between devices: 191 us -> 139 us
    all_to_all x0 -> x1, blocking collectives: none -> 74.7 us  [shards(): lax.all_to_all(jnp.stack([local_block for _ in range(lax.axis_size(IND))]...]
    all_gather x1 -> x0, waiting for transfers between devices: 53.3 us -> none  [shards(): lax.all_gather(white, IND, axis=0, tiled=True)]
  transfers between devices with their start and end apart: 7 -> 6, of which waited for: 5 -> 4; matrix products, arithmetic and copies ran while one was open for 3% -> 3% of each run, Pallas kernels for 0% -> 0%
where the time goes in v1:
time: 366 us; the launch traced here: 365 us
  waiting for transfers between devices  139 us (38%)
  blocking collectives  120 us (33%)
  matrix products  31.5 us (9%)
  local copies, waits for them, and re-layouts  27 us (7%)
  starting transfers between devices  21 us (6%)
  between operations  17.8 us (5%)
  other arithmetic  8.27 us (2%)
    reduce_scatter x3, waiting for transfers between devices, sum_in_order(): blocks = lax.psum_scatter(blocks, axes[k], scatter_dimension=0, tiled=True)  126 us
    all_to_all x1, blocking collectives, shards(): lax.all_to_all(jnp.stack([local_block for _ in range(lax.axis_size(IND))]...  74.7 us
    psum x5, blocking collectives, one_axis_at_a_time(): return functools.reduce(lax.psum, axes, array)  45.7 us
    all_to_all x3, starting transfers between devices, sent_to_all(): return lax.all_to_all(copies, axis, split_axis=0, concat_axis=0, tiled=True)  20.7 us
    dot_general x1, matrix products, cross_cov(): inner = jnp.dot(scaled_z, scaled_x.T, precision=lax.Precision.HIGHEST)  13.8 us
    all_to_all x3, waiting for transfers between devices, sent_to_all(): return lax.all_to_all(copies, axis, split_axis=0, concat_axis=0, tiled=True)  12.7 us
    convert_element_type x1, local copies, waits for them, and re-layouts, shards(): gram_part.astype(jnp.bfloat16)  12 us
    dot_general x1, matrix products, shards(): lax.dot_general(white, make_digits_all(white), (((1,), (1,)), ((), ())),...  8.9 us
  transfers between devices with their start and end apart: 6, of which 4 were waited for; matrix products, arithmetic and copies ran while one was open for 3% of the time, Pallas kernels for 0%

profile of v1, /device:TPU:1, one launch (start us, length us, event | category | flops | bytes accessed | tf_op | source)
XLA Modules:
  0.0 365.1 jit_solution(5458592160425357666)
XLA Ops:
  7.2 2.1 broadcast_in_dim.6
  9.3 6.7 %all-to-all-start = ((f32[4,1024,64]{1,2,0:T(8,128)}), f32[4,1024,64]{1,2,0:T(8,128)S(1)}, u32[]{:S(2)}, u32[]{:S(2)}) async-start(f32[4,1024,64]{1,2,0:T(8,128)} %broadcast_in_dim.6), calls=%async_computation | async-start | bytes 2097152 | tf_op jit(solution)/shard_map/all_to_all | solution.py:21
  16.0 1.3 fusion.15
  17.3 1.0 multiply_reduce_fusion.2
  18.3 12.7 %all-to-all-done = f32[4,1024,64]{1,2,0:T(8,128)S(1)} async-done(((f32[4,1024,64]{1,2,0:T(8,128)}), f32[4,1024,64]{1,2,0:T(8,128)S(1)}, u32[]{:S(2)}, u32[]{:S(2)}) %all-to-all-start) | async-done | bytes 1048608 | tf_op jit(solution)/shard_map/all_to_all | solution.py:21
  31.0 0.9 multiply_reduce_fusion.1
  32.0 13.8 %multiply_convert_fusion = bf16[4096,768]{1,0:T(8,128)(2,1)S(1)} fusion(f32[768]{0:T(1024)S(1)} %multiply_reduce_fusion.2, f32[4096]{0:T(1024)S(1)} %bitcast.46, f32[]{:T(128)} %bitcast, f32[4096,64]{0,1:T(8,128)S(1)} %bitcast.43, f32[64]{0:T(128)S(1)} %copy-done.6, bf16[768,64]{0,1:T(8,128)(2,1)S(1)} %copy-done.3), kind=kOutput, calls=%fused_computation | convolution fusion | flops 2435153920 | bytes 7458052 | tf_op jit(solution)/shard_map/dot_general | solution.py:68
  45.8 6.8 %multiply_reduce_fusion = (f32[768]{0:T(1024)S(1)}, bf16[768,1024]{1,0:T(8,128)(2,1)S(1)}) fusion(bf16[4096,768]{1,0:T(8,128)(2,1)S(1)} %multiply_convert_fusion, bf16[1024,4096]{1,0:T(8,128)(2,1)S(1)} %bitcast.48), kind=kOutput, calls=%fused_computation.2 | convolution fusion | flops 6445595648 | bytes 16256000 | tf_op jit(solution)/shard_map/dot_general | solution.py:90
  52.5 0.7 copy.32
  53.7 74.7 %all_to_all.22 = bf16[4,1024,768]{2,1,0:T(8,128)(2,1)S(1)} all-to-all(bf16[4,1024,768]{2,1,0:T(8,128)(2,1)S(1)} %stack.2), channel_id=1, replica_groups=mesh['dp_0'=8,'dp_1'=2,'rep'=4,'ind_0'=2,'ind_1'=2] {'ind_0','ind_1'}, dimensions={0} | all-to-all | bytes 12582912 | tf_op jit(solution)/shard_map/all_to_all | solution.py:95
  128.4 8.9 %convolution_convert_fusion = bf16[1024,4096]{1,0:T(8,128)(2,1)} fusion(bf16[768,1024]{1,0:T(8,128)(2,1)S(1)} %get-tuple-element.8, bf16[4096,768]{1,0:T(8,128)(2,1)S(1)} %bitcast.42), kind=kOutput, calls=%fused_computation.1 | convolution fusion | flops 6446645248 | bytes 16252928 | tf_op jit(solution)/shard_map/dot_general | solution.py:98
  137.3 12.0 %copy.33 = bf16[1024,4096]{0,1:T(8,128)(2,1)} copy(bf16[1024,4096]{1,0:T(8,128)(2,1)} %convolution_convert_fusion) | data formatting | bytes 16777216 | tf_op jit(solution)/shard_map/convert_element_type | solution.py:107
  149.2 8.4 %copy.34 = bf16[4,8,2,1024,64]{3,4,2,1,0:T(8,128)(2,1)} copy(bf16[4,8,2,1024,64]{3,4,0,2,1:T(8,128)(2,1)} %bitcast.39) | data formatting | bytes 16777216 | tf_op jit(solution)/shard_map/transpose | solution.py:43
  157.9 83.0 %reduce-scatter.4.cloned.1.call-done = bf16[16,1024,64]{1,2,0:T(8,128)(2,1)} async-done(((bf16[64,1024,64]{1,2,0:T(8,128)(2,1)}), bf16[16,1024,64]{1,2,0:T(8,128)(2,1)}) %reduce-scatter.4.cloned.1.call-update) | async-done | bytes 2097168 | tf_op jit(solution)/shard_map/reduce_scatter | solution.py:45
  241.0 1.3 convolution_reduce_fusion
  242.4 0.6 broadcast_in_dim.7
  243.0 5.0 %all-to-all-start.2 = ((f32[4,1,1536]{2,1,0:T(1,128)}), f32[4,1,1536]{2,1,0:T(1,128)S(1)}, u32[]{:S(2)}, u32[]{:S(2)}) async-start(f32[4,1,1536]{2,1,0:T(1,128)} %broadcast_in_dim.7), calls=%async_computation.5 | async-start | bytes 49152 | tf_op jit(solution)/shard_map/all_to_all | solution.py:21
  248.0 33.9 %reduce-scatter.6.cloned.1.call-done = bf16[2,1024,64]{1,2,0:T(8,128)(2,1)} async-done(((bf16[16,1024,64]{1,2,0:T(8,128)(2,1)}), bf16[2,1024,64]{1,2,0:T(8,128)(2,1)}) %reduce-scatter.6.cloned.1.call-update) | async-done | bytes 262160 | tf_op jit(solution)/shard_map/reduce_scatter | solution.py:45
  281.9 0.7 fusion.13
  282.7 1.2 fusion.9
  283.9 0.6 pad_maximum_fusion.1
  284.6 0.9 broadcast_in_dim.8
  285.4 9.1 %all-to-all-start.3 = ((f32[64,1,1025]{2,1,0:T(1,128)}), f32[64,1,1025]{2,1,0:T(1,128)S(1)}, u32[]{:S(2)}, u32[]{:S(2)}) async-start(f32[64,1,1025]{2,1,0:T(1,128)} %broadcast_in_dim.8), calls=%async_computation.6 | async-start | bytes 589824 | tf_op jit(solution)/shard_map/all_to_all | solution.py:21
  295.9 9.5 %reduce-scatter.8.cloned.1.call-done = bf16[1,1024,64]{1,2,0:T(8,128)(2,1)} async-done(((bf16[2,1024,64]{1,2,0:T(8,128)(2,1)}), bf16[1,1024,64]{1,2,0:T(8,128)(2,1)}) %reduce-scatter.8.cloned.1.call-update) | async-done | bytes 131088 | tf_op jit(solution)/shard_map/reduce_scatter | solution.py:45
  305.4 3.0 fusion.5
  308.4 14.2 %psum.35 = f32[]{:T(128)} all-reduce(f32[]{:T(128)} %get-tuple-element.3), channel_id=1, replica_groups=mesh['dp_0'=8,'dp_1'=2,'rep'=4,'ind_0'=2,'ind_1'=2] {'dp_0'}, use_global_device_ids=true, to_apply=%region_10.0 | all-reduce | flops 1 | bytes 8 | tf_op jit(solution)/shard_map/psum | solution.py:60
  322.6 4.4 %psum.36 = f32[]{:T(128)} all-reduce(f32[]{:T(128)} %psum.35), channel_id=1, replica_groups=mesh['dp_0'=8,'dp_1'=2,'rep'=4,'ind_0'=2,'ind_1'=2] {'dp_1'}, use_global_device_ids=true, to_apply=%region_11.0 | all-reduce | flops 1 | bytes 8 | tf_op jit(solution)/shard_map/psum | solution.py:60
  327.2 9.2 %psum.37 = f32[]{:T(128)} all-reduce(f32[]{:T(128)} %psum.36), channel_id=1, replica_groups=mesh['dp_0'=8,'dp_1'=2,'rep'=4,'ind_0'=2,'ind_1'=2] {'rep'}, use_global_device_ids=true, to_apply=%region_12.0 | all-reduce | flops 1 | bytes 8 | tf_op jit(solution)/shard_map/psum | solution.py:60
  336.4 1.2 fusion.8
  337.6 6.0 %psum.38 = f32[]{:T(128)} all-reduce(f32[]{:T(128)} %psum.37), channel_id=1, replica_groups=mesh['dp_0'=8,'dp_1'=2,'rep'=4,'ind_0'=2,'ind_1'=2] {'ind_0'}, use_global_device_ids=true, to_apply=%region_13.0 | all-reduce | flops 1 | bytes 8 | tf_op jit(solution)/shard_map/psum | solution.py:60
  343.6 0.5 slice.27
  344.1 11.9 %psum.39 = f32[]{:T(128)} all-reduce(f32[]{:T(128)} %psum.38), channel_id=1, replica_groups=mesh['dp_0'=8,'dp_1'=2,'rep'=4,'ind_0'=2,'ind_1'=2] {'ind_1'}, use_global_device_ids=true, to_apply=%region_14.0 | all-reduce | flops 1 | bytes 8 | tf_op jit(solution)/shard_map/psum | solution.py:60
  (36 shorter events, 1.1 us)
Async XLA Ops:
  7.2 233.9 %copy-start = (f32[1024]{0:T(1024)S(1)}, f32[1024]{0:T(1024)}, u32[]{:S(2)}) copy-start(f32[1024]{0:T(1024)} %param.14) | copy-start | bytes 12292
  7.2 24.7 %copy-start.6 = (f32[64]{0:T(128)S(1)}, f32[64]{0:T(128)}, u32[]{:S(2)}) copy-start(f32[64]{0:T(128)} %param.18) | copy-start | bytes 772
  7.2 24.7 %copy-start.3 = (bf16[768,64]{0,1:T(8,128)(2,1)S(1)}, bf16[768,64]{0,1:T(8,128)(2,1)}, u32[]{:S(2)}) copy-start(bf16[768,64]{0,1:T(8,128)(2,1)} %param.10) | copy-start | bytes 294916
  9.3 21.7 %all-to-all-start = ((f32[4,1024,64]{1,2,0:T(8,128)}), f32[4,1024,64]{1,2,0:T(8,128)S(1)}, u32[]{:S(2)}, u32[]{:S(2)}) async-start(f32[4,1024,64]{1,2,0:T(8,128)} %broadcast_in_dim.6), calls=%async_computation | async-start | bytes 2097152 | tf_op jit(solution)/shard_map/all_to_all | solution.py:21
  16.0 225.0 %reduce-scatter.4.cloned.1.call-start = ((), (), s32[]{:S(2)}) async-start(), calls=%async_computation.7 | async-start | bytes 10485760 | tf_op jit(solution)/shard_map/reduce_scatter | solution.py:45
  31.8 13.9 %slice-start = ((s8[8388608]{0:T(1024)(128)(4,1)}), s8[4194304]{0:T(1024)(128)(4,1)S(1)}, s32[]{:S(2)}) async-start(s8[8388608]{0:T(1024)(128)(4,1)} %bitcast.47), calls=%async_computation.10 | async-start | bytes 8388608
  31.9 13.8 %slice-start.1 = ((s8[8388608]{0:T(1024)(128)(4,1)}), s8[4194304]{0:T(1024)(128)(4,1)S(1)}, s32[]{:S(2)}) async-start(s8[8388608]{0:T(1024)(128)(4,1)} %bitcast.47), calls=%async_computation.11 | async-start | bytes 8388608
  157.6 83.4 %copy-start.4 = (f32[768]{0:T(1024)S(1)}, f32[768]{0:T(1024)}, u32[]{:S(2)}) copy-start(f32[768]{0:T(1024)} %param.11) | copy-start | bytes 9220
  157.6 147.8 %copy-start.1 = (f32[1024,64]{0,1:T(8,128)S(1)}, f32[1024,64]{0,1:T(8,128)}, u32[]{:S(2)}) copy-start(f32[1024,64]{0,1:T(8,128)} %param.15) | copy-start | bytes 786436
  157.6 147.8 %copy-start.2 = (f32[1024,64]{0,1:T(8,128)S(1)}, f32[1024,64]{0,1:T(8,128)}, u32[]{:S(2)}) copy-start(f32[1024,64]{0,1:T(8,128)} %param.16) | copy-start | bytes 786436
  157.6 178.8 %copy-start.5 = (f32[1024]{0:T(1024)S(1)}, f32[1024]{0:T(1024)}, u32[]{:S(2)}) copy-start(f32[1024]{0:T(1024)} %param.17) | copy-start | bytes 12292
  157.7 124.2 %reduce-scatter.6.cloned.1.call-start = ((), (), s32[]{:S(2)}) async-start(), calls=%async_computation.8 | async-start | bytes 2359296 | tf_op jit(solution)/shard_map/reduce_scatter | solution.py:45
  243.0 39.6 %all-to-all-start.2 = ((f32[4,1,1536]{2,1,0:T(1,128)}), f32[4,1,1536]{2,1,0:T(1,128)S(1)}, u32[]{:S(2)}, u32[]{:S(2)}) async-start(f32[4,1,1536]{2,1,0:T(1,128)} %broadcast_in_dim.7), calls=%async_computation.5 | async-start | bytes 49152 | tf_op jit(solution)/shard_map/all_to_all | solution.py:21
  248.0 57.4 %reduce-scatter.8.cloned.1.call-start = ((), (), s32[]{:S(2)}) async-start(), calls=%async_computation.9 | async-start | bytes 393216 | tf_op jit(solution)/shard_map/reduce_scatter | solution.py:45
  285.4 41.6 %all-to-all-start.3 = ((f32[64,1,1025]{2,1,0:T(1,128)}), f32[64,1,1025]{2,1,0:T(1,128)S(1)}, u32[]{:S(2)}, u32[]{:S(2)}) async-start(f32[64,1,1025]{2,1,0:T(1,128)} %broadcast_in_dim.8), calls=%async_computation.6 | async-start | bytes 589824 | tf_op jit(solution)/shard_map/all_to_all | solution.py:21
Sparse Core Ops, SparseCore 0:
  157.8 83.1 reduce-scatter.3
  243.5 38.3 reduce-scatter.5
  284.4 20.9 reduce-scatter.7
